TPU v7x, 256 devices: a whole 4x4x8 slice. The times are simulated.
256 devices in a mesh: section: 4 (over y_lo, core), expert: 64 (over y_hi, x, z).
Axes of the slice: x: 4, y: 4 (y_hi: 2, y_lo: 2; y = y_hi * 2 + y_lo), z: 8, core: 2. Of those that a mesh axis runs over, the one named last changes fastest.
Arguments:
- activations: bfloat16 [4, 2048, 4096], P('section', 'expert'), may hold values from -6 to 6
- norm_gain: float32 [4, 4096], P('section'), may hold values from 0.25 to 1.75
- in_proj: bfloat16 [4, 4096, 40960], P('section', None, 'expert'), may hold values from -0.09375 to 0.09375
- out_proj: bfloat16 [4, 40960, 4096], P('section', 'expert'), may hold values from -0.078125 to 0.078125
- expert_ids: int32 [4, 2048, 1], P('section', 'expert'), may hold values from 0 to 7; in each aligned block of 32 rows (0 to 31, 32 to 63, ..., all dimensions but the last counted through in order) at most 8 rows name the same one
Outputs:
- passed: bfloat16 [4, 2048, 4096], P('section', 'expert')
Inputs may be any that keep to these rules, and one draw needn't show every extreme that they name: `expert_ids`: within the 32 rows of one device (aligned blocks of 32 rows along the token dimension of each layer), no expert is named by more than 8 rows.
All inputs are finite; a program needn't handle non-finite values.
Results may differ from a plain program's by a relative error of at most 0.0047.
Values may be sent and summed in bfloat16 or wider, within the bound.
A program may use at most 64 MiB of HBM per device.

v0:
```python
import jax
import jax.numpy as jnp
from jax import lax
from jax.sharding import PartitionSpec as P

EXPERTS = 8


epsilon = 1e-06


def from_behind(block, axis, distance):
    devices = range(lax.axis_size(axis))
    route = [((i - distance) % len(devices), i) for i in devices]
    return lax.ppermute(block, axis, route)


def per_device(activations, norm_gain, in_proj, out_proj, expert_ids):
    floats = activations[0].astype(jnp.float32)
    tokens = floats.shape[0]
    width = floats.shape[1]
    scale = lax.rsqrt(jnp.mean(floats * floats, axis=-1, keepdims=True) + epsilon)
    normed = (floats * scale * norm_gain[0][None, :]).astype(jnp.bfloat16)
    groups = lax.axis_size("expert") // EXPERTS
    capacity = 2 * tokens // EXPERTS
    routed = expert_ids[0, :, 0]
    onehot = (routed[:, None] == jnp.arange(EXPERTS, dtype=jnp.int32)[None, :]).astype(jnp.int32)
    before = jnp.cumsum(onehot, axis=0) - onehot
    ranks = jnp.sum(before * onehot, axis=1)
    slot_index = routed * capacity + ranks
    placing = jnp.arange(EXPERTS * capacity, dtype=jnp.int32)[:, None] == slot_index[None, :]
    packed = jnp.dot(
        placing.astype(jnp.bfloat16), normed, preferred_element_type=jnp.float32
    ).astype(jnp.bfloat16)
    first_proj = in_proj[0]
    second_proj = out_proj[0]
    outgoing = jnp.repeat(packed.reshape(EXPERTS, capacity, width), groups, axis=0)
    received = lax.all_to_all(outgoing, "expert", split_axis=0, concat_axis=0, tiled=True)
    flat = received.reshape(received.shape[0] * received.shape[1], width)
    preact = jnp.dot(flat, first_proj, preferred_element_type=jnp.float32)
    hidden = jax.nn.gelu(preact, approximate=True).astype(jnp.bfloat16)
    piece = jnp.dot(hidden, second_proj, preferred_element_type=jnp.float32)
    returned = lax.all_to_all(
        piece.reshape(received.shape[0], received.shape[1], width).astype(jnp.bfloat16),
        "expert",
        split_axis=0,
        concat_axis=0,
        tiled=True,
    ).astype(jnp.float32)
    combined = jnp.sum(returned.reshape(EXPERTS, groups, capacity, width), axis=1)
    mixed_rows = jnp.dot(
        placing.T.astype(jnp.float32),
        combined.reshape(EXPERTS * capacity, width),
        precision=lax.Precision.HIGHEST,
        preferred_element_type=jnp.float32,
    )
    updated = (floats + mixed_rows).astype(jnp.bfloat16)
    return from_behind(updated[None], "section", 1)


def solution(mesh):
    return jax.shard_map(
        per_device,
        mesh=mesh,
        in_specs=(
            P("section", "expert", None),
            P("section", None),
            P("section", None, "expert"),
            P("section", "expert", None),
            P("section", "expert", None),
        ),
        out_specs=P("section", "expert", None),
        check_vma=False,
    )
```

profile of v0, /device:TPU:1, one launch (start us, length us, event | category | flops | bytes accessed | tf_op | source)
XLA Modules:
  0.0 233.7 jit_solution(14836267829743901081)
XLA Ops:
  0.0 1.1 fusion.25
  1.1 0.7 fusion.34
  1.9 0.1 reduce_window_sum.11
  1.9 0.8 select_reduce_fusion
  2.7 0.7 multiply_add_fusion
  3.4 1.3 fusion.3
  4.7 0.0 slice-start
  4.7 0.5 broadcast_in_dim.4
  5.3 0.0 slice-start.1
  5.3 0.0 slice-start.2
  5.3 109.2 %all_to_all.10 = bf16[64,8,4096]{2,1,0:T(8,128)(2,1)S(1)} all-to-all(bf16[64,8,4096]{2,1,0:T(8,128)(2,1)S(1)} %bitcast.43), channel_id=1, replica_groups=mesh['section'=4,'expert'=64] {'expert'}, dimensions={0} | all-to-all | bytes 8388608 | tf_op jit(solution)/shard_map/all_to_all | solution.py:38
  114.5 0.0 slice-done
  114.5 0.0 slice-done.1
  114.5 0.0 slice-start.3
  114.5 3.5 %fusion.19 = bf16[64,8,640]{2,1,0:T(8,128)(2,1)S(1)} fusion(bf16[1,4096,640]{2,1,0:T(8,128)(2,1)S(1)} %bitcast.48, bf16[64,8,4096]{2,1,0:T(8,128)(2,1)S(1)} %all_to_all.10), kind=kOutput, calls=%fused_computation.20 | convolution fusion | flops 2687303680 | bytes 10092544 | tf_op jit(solution)/shard_map/dot_general | solution.py:40
  118.0 0.0 slice-done.2
  118.1 0.0 slice-done.3
  118.1 3.7 %convolution_convert_fusion = bf16[64,8,4096]{2,1,0:T(8,128)(2,1)S(1)} fusion(bf16[64,8,640]{2,1,0:T(8,128)(2,1)S(1)} %fusion.19, bf16[1,640,4096]{2,1,0:T(8,128)(2,1)S(1)} %bitcast.50), kind=kOutput, calls=%fused_computation.1 | convolution fusion | flops 2686451712 | bytes 10092544 | tf_op jit(solution)/shard_map/dot_general | solution.py:42
  121.8 102.0 %all_to_all.11 = bf16[64,8,4096]{2,1,0:T(8,128)(2,1)S(1)} all-to-all(bf16[64,8,4096]{2,1,0:T(8,128)(2,1)S(1)} %convolution_convert_fusion), channel_id=1, replica_groups=mesh['section'=4,'expert'=64] {'expert'}, dimensions={0} | all-to-all | bytes 8388608 | tf_op jit(solution)/shard_map/all_to_all | solution.py:43
  223.8 0.0 copy-start
  223.8 0.7 convert_reduce_fusion
  224.5 0.3 copy-done
  224.8 0.5 fusion.5
  225.3 4.4 %collective-permute-start = (bf16[1,32,4096]{2,1,0:T(8,128)(2,1)S(1)}, bf16[1,32,4096]{2,1,0:T(8,128)(2,1)S(1)}, u32[]{:S(2)}, u32[]{:S(2)}) collective-permute-start(bf16[1,32,4096]{2,1,0:T(8,128)(2,1)S(1)} %fusion.5), channel_id=1, source_target_pairs={{192,0},{0,64},{64,128},{128,192},{193,1},{1,65},{65,129},{129,193... | collective-permute-start | bytes 786440 | tf_op jit(solution)/shard_map/ppermute | solution.py:15
  229.7 3.3 %collective-permute-done = bf16[1,32,4096]{2,1,0:T(8,128)(2,1)S(1)} collective-permute-done((bf16[1,32,4096]{2,1,0:T(8,128)(2,1)S(1)}, bf16[1,32,4096]{2,1,0:T(8,128)(2,1)S(1)}, u32[]{:S(2)}, u32[]{:S(2)}) %collective-permute-start) | collective-permute-done | bytes 262176 | tf_op jit(solution)/shard_map/ppermute | solution.py:15
  233.0 0.7 copy.7
  (3 shorter events, 0.0 us)
Async XLA Ops:
  4.7 109.8 %slice-start = ((s8[5242880]{0:T(1024)(128)(4,1)}), s8[4194304]{0:T(1024)(128)(4,1)S(1)}, s32[]{:S(2)}) async-start(s8[5242880]{0:T(1024)(128)(4,1)} %bitcast.47), calls=%async_computation.2 | async-start | bytes 8388608
  5.3 109.2 %slice-start.1 = ((s8[5242880]{0:T(1024)(128)(4,1)}), s8[1048576]{0:T(1024)(128)(4,1)S(1)}, s32[]{:S(2)}) async-start(s8[5242880]{0:T(1024)(128)(4,1)} %bitcast.47), calls=%async_computation.3 | async-start | bytes 2097152
  5.3 112.8 %slice-start.2 = ((s8[5242880]{0:T(1024)(128)(4,1)}), s8[4194304]{0:T(1024)(128)(4,1)S(1)}, s32[]{:S(2)}) async-start(s8[5242880]{0:T(1024)(128)(4,1)} %bitcast.49), calls=%async_computation.4 | async-start | bytes 8388608
  114.5 3.6 %slice-start.3 = ((s8[5242880]{0:T(1024)(128)(4,1)}), s8[1048576]{0:T(1024)(128)(4,1)S(1)}, s32[]{:S(2)}) async-start(s8[5242880]{0:T(1024)(128)(4,1)} %bitcast.49), calls=%async_computation.5 | async-start | bytes 2097152
  223.8 1.0 copy-start
  225.3 7.7 %collective-permute-start = (bf16[1,32,4096]{2,1,0:T(8,128)(2,1)S(1)}, bf16[1,32,4096]{2,1,0:T(8,128)(2,1)S(1)}, u32[]{:S(2)}, u32[]{:S(2)}) collective-permute-start(bf16[1,32,4096]{2,1,0:T(8,128)(2,1)S(1)} %fusion.5), channel_id=1, source_target_pairs={{192,0},{0,64},{64,128},{128,192},{193,1},{1,65},{65,129},{129,193... | collective-permute-start | bytes 786440 | tf_op jit(solution)/shard_map/ppermute | solution.py:15
where the time goes:
time: 236 us; the launch traced here: 234 us
  blocking collectives  211 us (89%)
  matrix products  9.05 us (4%)
  starting transfers between devices  4.4 us (2%)
  other arithmetic  4.08 us (2%)
  waiting for transfers between devices  3.32 us (1%)
    all_to_all x1, blocking collectives, per_device(): lax.all_to_all(outgoing, 'expert', split_axis=0, concat_axis=0, tiled=True)  109 us
    all_to_all x1, blocking collectives, per_device(): lax.all_to_all(piece.reshape(received.shape[0], received.shape[1], width)...  102 us
  transfers between devices with their start and end apart: 1, of which 1 were waited for; matrix products, arithmetic and copies ran while one was open for 0% of the time, Pallas kernels for 0%

commit v1 on v0

v1 whole, which is shorter than its diff:
```python
import functools

import jax
import jax.numpy as jnp
from jax import lax
from jax.experimental import pallas as pl
from jax.experimental.pallas import tpu as pltpu
from jax.sharding import PartitionSpec as P

MESH = pl.DeviceIdType.MESH
EPS = 1e-06
NZ = 8
NR = 8
NX = 4
CAP = 8
ROWS = NR * CAP
CA = 2048
CHUNK = 1024

ZI = {0: 0, 1: 1, -1: 2, 2: 3, -2: 4, 3: 5, -3: 6, 4: 7, -4: 7}
FAR = {(1, 0): 4, (1, 1): 3, (-1, 0): 3, (-1, 1): 4}
CHAINS = [(1, 0), (1, 1), (-1, 0), (-1, 1)]


def opposite(r):
    return r // NX * NX + (NX - r % NX) % NX


def kernel(
    act, gain, ids, w1_hbm, w2_hbm, out,
    w1, w2, codes, gathered, packed_a, packed_b, xa, xb, pre, own_a, back_b,
    ret_b, own_b, sum_a, ret_a, final,
    send_a, land_a, send_b, land_b,
    w_sem, one_send, one_recv, ag_recv, plane_recv, rs_recv,
):
    tokens, width = act.shape
    cb = width - CA
    s = lax.axis_index("section")
    e = lax.axis_index("expert")
    z, p = lax.rem(e, NZ), e // NZ
    yh, x = p // NX, lax.rem(p, NX)

    def z_dev(k):
        return (s, p * NZ + lax.rem(z + k + NZ, NZ))

    def plane_of(r):
        return lax.rem(yh + r // NX, NR // NX) * NX + lax.rem(x + r % NX, NX)

    def r_dev(r):
        return (s, plane_of(r) * NZ + z)

    sections = lax.axis_size("section")
    ahead = (lax.rem(s + 1, sections), e)
    behind = (lax.rem(s + sections - 1, sections), e)

    def remote(src, dst, send, recv, to):
        return pltpu.make_async_remote_copy(
            src_ref=src, dst_ref=dst, send_sem=send, recv_sem=recv,
            device_id=to, device_id_type=MESH,
        )

    def drain(ref, sem):
        pltpu.make_async_copy(ref, ref, sem).wait()

    load_w1 = pltpu.make_async_copy(w1_hbm, w1, w_sem.at[0])
    load_w2 = pltpu.make_async_copy(w2_hbm, w2, w_sem.at[1])
    load_w1.start()
    load_w2.start()

    barrier = pltpu.get_barrier_semaphore()
    peers = [r_dev(r) for r in range(1, NR)] + [z_dev(k) for k in range(1, NZ)]
    for to in peers + [ahead, behind]:
        pl.semaphore_signal(barrier, inc=1, device_id=to, device_id_type=MESH)

    floats = act[...].astype(jnp.float32)
    scale = lax.rsqrt(jnp.mean(floats * floats, axis=-1, keepdims=True) + EPS)
    normed = (floats * scale * gain[...]).astype(jnp.bfloat16)
    gathered[0] = normed[:, CA:]

    col = jnp.broadcast_to(ids[...], (tokens, 128))[:, :tokens]
    i0 = lax.broadcasted_iota(jnp.int32, (tokens, tokens), 0)
    i1 = lax.broadcasted_iota(jnp.int32, (tokens, tokens), 1)
    row = jnp.sum(jnp.where(i0 == i1, col, 0), axis=0, keepdims=True)
    rank = jnp.sum(
        jnp.where((col == row) & (i0 < i1), 1, 0), axis=0, keepdims=True
    )
    code = row * CAP + rank
    codes[0, :, 0:tokens] = jnp.broadcast_to(code, (8, tokens))

    slot = lax.broadcasted_iota(jnp.int32, (ROWS, tokens), 0)
    rel = slot // CAP
    expert_of = lax.rem(yh + rel // NX, NR // NX) * NX + lax.rem(x + lax.rem(rel, NX), NX)
    wanted = expert_of * CAP + lax.rem(slot, CAP)

    def placing(i):
        return jnp.where(wanted == codes[i, 0:1, 0:tokens], 1.0, 0.0).astype(jnp.bfloat16)

    def pack(place, rows):
        return jnp.dot(place, rows, preferred_element_type=jnp.float32).astype(jnp.bfloat16)

    def unpack(place, slots):
        return lax.dot_general(
            place, slots, (((0,), (0,)), ((), ())), preferred_element_type=jnp.float32
        )

    place_own = jnp.where(wanted == code, 1.0, 0.0).astype(jnp.bfloat16)
    packed_a[...] = pack(place_own, normed[:, :CA]).reshape(NR, CAP, CA)

    pl.semaphore_wait(barrier, len(peers) + 2)

    def ag_copy(buf, kind, d, h, k, cols):
        half = cols // 2
        at = pl.ds(h * half, half)
        if kind == 0:
            src, dst = buf.at[ZI[d * k], :, :, at], buf.at[ZI[d * (k + 1)], :, :, at]
        else:
            src, dst = buf.at[ZI[d * k], :, at], buf.at[ZI[d * (k + 1)], :, at]
        chain = CHAINS.index((d, h))
        return remote(
            src, dst, one_send.at[kind], ag_recv.at[kind, chain, k], z_dev(d)
        )

    def ag_a(d, h, k):
        return ag_copy(xa, 0, d, h, k, CA)

    def ag_b(d, h, k):
        return ag_copy(gathered, 1, d, h, k, cb)

    def forward(ag, k):
        for d, h in CHAINS:
            if k <= FAR[d, h]:
                ag(d, h, k - 1).wait_recv()
                if k < FAR[d, h]:
                    ag(d, h, k).start()

    for d, h in CHAINS:
        ag_b(d, h, 0).start()
    for k in range(1, NZ):
        remote(codes.at[0], codes.at[NZ - k], one_send.at[2], one_recv.at[0], z_dev(k)).start()

    for r in range(1, NR):
        remote(
            packed_a.at[r], xa.at[0, opposite(r)], one_send.at[3], one_recv.at[1], r_dev(r)
        ).start()
    xa[0, 0] = packed_a[0]

    def send_packed(i, place):
        packed_b[i] = pack(place, gathered[i]).reshape(NR, CAP, cb)
        for r in range(1, NR):
            remote(
                packed_b.at[i, r], xb.at[i, opposite(r)],
                one_send.at[4], plane_recv.at[0, i], r_dev(r),
            ).start()
        xb[i, 0] = packed_b[i, 0]

    send_packed(0, place_own)
    drain(xa.at[0, pl.ds(1, NR - 1)], one_recv.at[1])
    for d, h in CHAINS:
        ag_a(d, h, 0).start()
    forward(ag_b, 1)
    drain(codes.at[pl.ds(1, NZ - 1)], one_recv.at[0])

    def place_of(i):
        k = [d for d in range(-3, 5) if ZI[d] == i][0]
        return placing((-k) % NZ)

    for i in (1, 2):
        send_packed(i, place_of(i))
    forward(ag_b, 2)
    for i in (3, 4):
        send_packed(i, place_of(i))
    forward(ag_a, 1)
    load_w1.wait()
    load_w2.wait()

    def ffn(i, n):
        rows = n * ROWS
        for c in range(0, width, CHUNK):
            if c < CA:
                block = xa[i:i + n, :, :, c:c + CHUNK]
            else:
                block = xb[i:i + n, :, :, c - CA:c - CA + CHUNK]
            term = jnp.dot(
                block.reshape(rows, CHUNK), w1[c:c + CHUNK, :],
                preferred_element_type=jnp.float32,
            )
            if c == 0:
                pre[0:rows, :] = term
            else:
                pre[0:rows, :] += term
        hidden = jax.nn.gelu(pre[0:rows, :], approximate=True).astype(jnp.bfloat16)
        for c in range(0, width, CHUNK):
            part = jnp.dot(
                hidden, w2[:, c:c + CHUNK], preferred_element_type=jnp.float32
            )
            if c < CA:
                own_a[i:i + n, :, c:c + CHUNK] = part.reshape(n, ROWS, CHUNK)
            else:
                back_b[i:i + n, :, :, c - CA:c - CA + CHUNK] = (
                    part.astype(jnp.bfloat16).reshape(n, NR, CAP, CHUNK)
                )

    def run(i, n):
        for j in range(i, i + n):
            drain(xb.at[j, pl.ds(1, NR - 1)], plane_recv.at[0, j])
        ffn(i, n)
        for j in range(i, i + n):
            for r in range(1, NR):
                remote(
                    back_b.at[j, r], ret_b.at[j, opposite(r)],
                    one_send.at[5], plane_recv.at[1, j], r_dev(r),
                ).start()
            ret_b[j, 0] = back_b[j, 0]

    run(0, 1)
    forward(ag_b, 3)
    for i in (5, 6):
        send_packed(i, place_of(i))
    forward(ag_a, 2)
    run(1, 2)
    forward(ag_b, 4)
    send_packed(7, place_of(7))
    forward(ag_a, 3)
    run(3, 2)
    forward(ag_a, 4)

    def rs_copy(kind, d, h, k):
        send, land = ((send_a, land_a), (send_b, land_b))[kind]
        chain = CHAINS.index((d, h))
        return remote(
            send.at[chain, k - 1], land.at[chain, k - 1],
            one_send.at[6 + kind], rs_recv.at[kind, chain, k - 1], z_dev(-d),
        )

    def rs_own(kind, d, h, k):
        own, cols = ((own_a, CA), (own_b, cb))[kind]
        half = cols // 2
        return own[ZI[d * k], :, h * half:(h + 1) * half]

    def rs_head(kind, k):
        for d, h in CHAINS:
            if k == FAR[d, h]:
                send = (send_a, send_b)[kind]
                send[CHAINS.index((d, h)), k - 1] = rs_own(kind, d, h, k).astype(jnp.bfloat16)
                rs_copy(kind, d, h, k).start()

    def rs_step(kind, k):
        send, land = ((send_a, land_a), (send_b, land_b))[kind]
        for d, h in CHAINS:
            if k < FAR[d, h]:
                chain = CHAINS.index((d, h))
                rs_copy(kind, d, h, k + 1).wait_recv()
                send[chain, k - 1] = (
                    rs_own(kind, d, h, k) + land[chain, k].astype(jnp.float32)
                ).astype(jnp.bfloat16)
                rs_copy(kind, d, h, k).start()

    def rs_last(kind, h):
        land = (land_a, land_b)[kind]
        total = rs_own(kind, 1, h, 0)
        for d in (1, -1):
            rs_copy(kind, d, h, 1).wait_recv()
            total = total + land[CHAINS.index((d, h)), 0].astype(jnp.float32)
        return total

    def take_b(i):
        drain(ret_b.at[i, pl.ds(1, NR - 1)], plane_recv.at[1, i])
        own_b[i] = unpack(place_of(i), ret_b[i].reshape(ROWS, cb))

    run(5, 2)
    rs_head(0, 3)
    run(7, 1)
    rs_head(0, 4)
    rs_step(0, 3)
    rs_step(0, 2)
    for i in (5, 6):
        take_b(i)
    rs_head(1, 3)
    take_b(7)
    rs_head(1, 4)
    rs_step(0, 1)
    for i in (3, 4):
        take_b(i)
    rs_step(1, 3)
    half = CA // 2
    for h in range(2):
        sum_a[:, :, h * half:(h + 1) * half] = (
            rs_last(0, h).astype(jnp.bfloat16).reshape(NR, CAP, half)
        )
    for r in range(1, NR):
        remote(
            sum_a.at[r], ret_a.at[opposite(r)], one_send.at[8], one_recv.at[2], r_dev(r)
        ).start()
    ret_a[0] = sum_a[0]
    rs_step(1, 2)
    for i in (1, 2):
        take_b(i)
    rs_step(1, 1)
    take_b(0)

    drain(ret_a.at[pl.ds(1, NR - 1)], one_recv.at[2])
    final[:, :CA] = (
        act[:, :CA].astype(jnp.float32) + unpack(place_own, ret_a[...].reshape(ROWS, CA))
    ).astype(jnp.bfloat16)
    out_a = remote(
        final.at[:, pl.ds(0, CA)], out.at[:, pl.ds(0, CA)], one_send.at[9], one_recv.at[3], ahead
    )
    out_a.start()
    half = cb // 2
    for h in range(2):
        at = slice(CA + h * half, CA + (h + 1) * half)
        final[:, at] = (act[:, at].astype(jnp.float32) + rs_last(1, h)).astype(jnp.bfloat16)
    out_b = remote(
        final.at[:, pl.ds(CA, cb)], out.at[:, pl.ds(CA, cb)], one_send.at[10], one_recv.at[4], ahead
    )
    out_b.start()

    drain(xa.at[pl.ds(1, NZ - 1)], one_send.at[0])
    drain(gathered.at[pl.ds(1, NZ - 1)], one_send.at[1])
    drain(codes.at[pl.ds(1, NZ - 1)], one_send.at[2])
    drain(packed_a.at[pl.ds(1, NR - 1)], one_send.at[3])
    drain(packed_b.at[:, pl.ds(1, NR - 1)], one_send.at[4])
    drain(back_b.at[:, pl.ds(1, NR - 1)], one_send.at[5])
    drain(xa.at[pl.ds(1, NZ - 1)], one_send.at[6])
    drain(gathered.at[pl.ds(1, NZ - 1)], one_send.at[7])
    drain(sum_a.at[pl.ds(1, NR - 1)], one_send.at[8])
    out_a.wait()
    out_b.wait()


def per_device(activations, norm_gain, in_proj, out_proj, expert_ids):
    _, tokens, width = activations.shape
    hidden = in_proj.shape[2]
    cb = width - CA
    bf16, f32 = jnp.bfloat16, jnp.float32
    vmem = pl.BlockSpec(memory_space=pltpu.VMEM)
    hbm = pl.BlockSpec(memory_space=pl.ANY)
    out = pl.pallas_call(
        kernel,
        out_shape=jax.ShapeDtypeStruct((tokens, width), bf16),
        in_specs=[vmem, vmem, vmem, hbm, hbm],
        out_specs=vmem,
        scratch_shapes=[
            pltpu.VMEM((width, hidden), bf16),
            pltpu.VMEM((hidden, width), bf16),
            pltpu.VMEM((NZ, 8, 128), jnp.int32),
            pltpu.VMEM((NZ, tokens, cb), bf16),
            pltpu.VMEM((NR, CAP, CA), bf16),
            pltpu.VMEM((NZ, NR, CAP, cb), bf16),
            pltpu.VMEM((NZ, NR, CAP, CA), bf16),
            pltpu.VMEM((NZ, NR, CAP, cb), bf16),
            pltpu.VMEM((2 * ROWS, hidden), f32),
            pltpu.VMEM((NZ, ROWS, CA), f32),
            pltpu.VMEM((NZ, NR, CAP, cb), bf16),
            pltpu.VMEM((NZ, NR, CAP, cb), bf16),
            pltpu.VMEM((NZ, tokens, cb), f32),
            pltpu.VMEM((NR, CAP, CA), bf16),
            pltpu.VMEM((NR, CAP, CA), bf16),
            pltpu.VMEM((tokens, width), bf16),
            pltpu.VMEM((4, 4, ROWS, CA // 2), bf16),
            pltpu.VMEM((4, 4, ROWS, CA // 2), bf16),
            pltpu.VMEM((4, 4, tokens, cb // 2), bf16),
            pltpu.VMEM((4, 4, tokens, cb // 2), bf16),
            pltpu.SemaphoreType.DMA((2,)),
            pltpu.SemaphoreType.DMA((11,)),
            pltpu.SemaphoreType.DMA((5,)),
            pltpu.SemaphoreType.DMA((2, 4, 4)),
            pltpu.SemaphoreType.DMA((2, NZ)),
            pltpu.SemaphoreType.DMA((2, 4, 4)),
        ],
        compiler_params=pltpu.CompilerParams(
            collective_id=0, has_side_effects=True, vmem_limit_bytes=58 * 2**20
        ),
    )(activations[0], norm_gain, expert_ids[0], in_proj[0], out_proj[0])
    return out[None]


def solution(mesh):
    return jax.shard_map(
        per_device,
        mesh=mesh,
        in_specs=(
            P("section", "expert", None),
            P("section", None),
            P("section", None, "expert"),
            P("section", "expert", None),
            P("section", "expert", None),
        ),
        out_specs=P("section", "expert", None),
        check_vma=False,
    )
```

time: 236 us -> 96.8 us (0.41)
  blocking collectives: 211 us -> 0 us
  Pallas kernels: 0 us -> 93.6 us
  matrix products: 9.05 us -> 0 us
  starting transfers between devices: 4.4 us -> 0 us
  other arithmetic: 4.08 us -> 0 us
  waiting for transfers between devices: 3.32 us -> 0 us
    all_to_all x2 -> x0, blocking collectives: 211 us -> none  [the longest x1 109 us: per_device(): lax.all_to_all(outgoing, 'expert', split_axis=0, concat_axis=0, tiled=True)]
    pallas_call x0 -> x1, Pallas kernels: none -> 93.6 us  [per_device(): pl.pallas_call(kernel, out_shape=jax.ShapeDtypeStruct((tokens, width), bf...]
    dot_general x4 -> x0, matrix products: 9.05 us -> none  [the longest x1 3.69 us: per_device(): piece = jnp.dot(hidden, second_proj, preferred_element_type=jnp.float32)]
    ppermute x1 -> x0, starting transfers between devices: 4.4 us -> none  [from_behind(): return lax.ppermute(block, axis, route)]
    ppermute x1 -> x0, waiting for transfers between devices: 3.32 us -> none  [from_behind(): return lax.ppermute(block, axis, route)]
    reduce_sum x3 -> x0, other arithmetic: 2.62 us -> none  [the longest x1 1.11 us: per_device(): jnp.mean(floats * floats, axis=-1, keepdims=True) + epsilon]
  transfers between devices with their start and end apart: 1 -> 0, of which waited for: 1 -> 0; matrix products, arithmetic and copies ran while one was open for 0% -> 0% of each run, Pallas kernels for 0% -> 0%
where the time goes in v1:
time: 96.8 us; the launch traced here: 96.7 us
  Pallas kernels  93.6 us (97%)
  local copies, waits for them, and re-layouts  3.01 us (3%)
    pallas_call x1, Pallas kernels, per_device(): pl.pallas_call(kernel, out_shape=jax.ShapeDtypeStruct((tokens, width), bf...  93.6 us

profile of v1, /device:TPU:1, one launch (start us, length us, event | category | flops | bytes accessed | tf_op | source)
XLA Modules:
  0.0 96.7 jit_solution(5481717926961603711)
XLA Ops:
  0.0 1.3 %copy.6.ids = s32[32,1]{1,0:T(8,128)} copy(s32[32,1]{0,1:T(1,128)} %bitcast.9) | data formatting | bytes 256 | tf_op jit(solution)/shard_map/squeeze | solution.py:374
  1.3 93.6 %shard_map.55 = bf16[32,4096]{1,0:T(8,128)(2,1)} custom-call(bf16[32,4096]{1,0:T(8,128)(2,1)} %bitcast.8, f32[1,4096]{1,0:T(1,128)} %gain.1, s32[32,1]{1,0:T(8,128)} %copy.6.ids, bf16[4096,640]{1,0:T(8,128)(2,1)} %bitcast.5, bf16[640,4096]{1,0:T(8,128)(2,1)} %bitcast.6), custom_call_target="tpu_custom_call" | custom-call | tf_op jit(solution)/shard_map/pallas_call | solution.py:338
  95.0 1.7 %copy.8 = bf16[1,32,4096]{2,1,0:T(8,128)(2,1)} copy(bf16[1,32,4096]{2,1,0:T(8,128)(2,1)} %bitcast.7) | data formatting | bytes 524288

commit v2 on v1

v2 whole, which is shorter than its diff:
```python
import functools

import jax
import jax.numpy as jnp
from jax import lax
from jax.experimental import pallas as pl
from jax.experimental.pallas import tpu as pltpu
from jax.sharding import PartitionSpec as P

MESH = pl.DeviceIdType.MESH
EPS = 1e-06
NZ = 8
NR = 8
NX = 4
CAP = 8
GROUPS = 2
PART = NR // GROUPS
ROWS = NR * CAP
CA = 2048
CHUNK = 1024

ZI = {0: 0, 1: 1, -1: 2, 2: 3, -2: 4, 3: 5, -3: 6, 4: 7, -4: 7}
FAR = {(1, 0): 4, (1, 1): 3, (-1, 0): 3, (-1, 1): 4}
CHAINS = [(1, 0), (-1, 1), (1, 1), (-1, 0)]


def opposite(r):
    return r // NX * NX + (NX - r % NX) % NX


def kernel(
    act_hbm, gain_hbm, ids_hbm, w1_hbm, w2_hbm, out,
    act, gain, ids, before, w1, w2, codes, gathered, packed_a, packed_b, xa, xb, pre, own_a, back_b,
    ret_b, own_b, sum_a, ret_a, tail_b,
    send_a, land_a, send_b, land_b,
    w_sem, one_send, one_recv, ag_recv, plane_recv, rs_recv,
):
    tokens, width = act_hbm.shape
    cb = width - CA
    s = lax.axis_index("section")
    e = lax.axis_index("expert")
    z, p = lax.rem(e, NZ), e // NZ
    yh, x = p // NX, lax.rem(p, NX)

    def z_dev(k, section=s):
        return (section, p * NZ + lax.rem(z + k + NZ, NZ))

    def plane_of(r):
        return lax.rem(yh + r // NX, NR // NX) * NX + lax.rem(x + r % NX, NX)

    def r_dev(r, section=s):
        return (section, plane_of(r) * NZ + z)

    sections = lax.axis_size("section")
    ahead, behind = lax.rem(s + 1, sections), lax.rem(s + sections - 1, sections)

    def remote(src, dst, send, recv, to):
        return pltpu.make_async_remote_copy(
            src_ref=src, dst_ref=dst, send_sem=send, recv_sem=recv,
            device_id=to, device_id_type=MESH,
        )

    def drain(ref, sem):
        pltpu.make_async_copy(ref, ref, sem).wait()

    barrier = pltpu.get_barrier_semaphore()
    peers = [r_dev(r) for r in range(1, NR)] + [z_dev(k) for k in range(1, NZ)]
    peers += [r_dev(r, behind) for r in range(NR)] + [z_dev(k, behind) for k in (1, -1)]
    for to in peers:
        pl.semaphore_signal(barrier, inc=1, device_id=to, device_id_type=MESH)

    loads = [
        pltpu.make_async_copy(src, dst, w_sem.at[i])
        for i, (src, dst) in enumerate(
            [(act_hbm, act), (gain_hbm, gain), (ids_hbm, ids), (w1_hbm, w1), (w2_hbm, w2)]
        )
    ]
    for load in loads:
        load.start()
    for load in loads[:3]:
        load.wait()

    floats = act[...].astype(jnp.float32)
    scale = lax.rsqrt(jnp.mean(floats * floats, axis=-1, keepdims=True) + EPS)
    normed = (floats * scale * gain[...]).astype(jnp.bfloat16)
    gathered[0] = normed[:, CA:]

    i0 = lax.broadcasted_iota(jnp.int32, (tokens, tokens), 0)
    i1 = lax.broadcasted_iota(jnp.int32, (tokens, tokens), 1)
    row = ids[...]
    col = jnp.sum(jnp.where(i0 == i1, row, 0), axis=1, keepdims=True)
    rank = jnp.sum(
        jnp.where((col == row) & (i0 < i1), 1, 0), axis=0, keepdims=True
    )
    code = row * CAP + rank
    codes[0, :, 0:tokens] = jnp.broadcast_to(code, (8, tokens))

    slot = lax.broadcasted_iota(jnp.int32, (ROWS, tokens), 0)
    rel = slot // CAP
    expert_of = lax.rem(yh + rel // NX, NR // NX) * NX + lax.rem(x + lax.rem(rel, NX), NX)
    wanted = expert_of * CAP + lax.rem(slot, CAP)

    def placing(i):
        return jnp.where(wanted == codes[i, 0:1, 0:tokens], 1.0, 0.0).astype(jnp.bfloat16)

    def pack(place, rows):
        return jnp.dot(place, rows, preferred_element_type=jnp.float32).astype(jnp.bfloat16)

    def unpack(place, slots):
        return lax.dot_general(
            place, slots, (((0,), (0,)), ((), ())), preferred_element_type=jnp.float32
        )

    place_own = jnp.where(wanted == code, 1.0, 0.0).astype(jnp.bfloat16)
    packed_a[...] = pack(place_own, normed[:, :CA]).reshape(NR, CAP, CA)

    pl.semaphore_wait(barrier, len(peers))

    def ag_copy(kind, d, h, k):
        chain = CHAINS.index((d, h))
        if kind < GROUPS:
            at = pl.ds(h * CA // 2, CA // 2)
            rows = pl.ds(kind * PART, PART)
            src, dst = xa.at[ZI[d * k], rows, :, at], xa.at[ZI[d * (k + 1)], rows, :, at]
        else:
            at = pl.ds(h * cb // 2, cb // 2)
            src, dst = gathered.at[ZI[d * k], :, at], gathered.at[ZI[d * (k + 1)], :, at]
        return remote(
            src, dst, one_send.at[kind // GROUPS], ag_recv.at[kind, chain, k], z_dev(d)
        )

    def begin(kind):
        for d, h in CHAINS:
            ag_copy(kind, d, h, 0).start()

    def forward(kind, k):
        for d, h in CHAINS:
            if k <= FAR[d, h]:
                ag_copy(kind, d, h, k - 1).wait_recv()
                if k < FAR[d, h]:
                    ag_copy(kind, d, h, k).start()

    begin(2)

    for r in range(1, NR):
        remote(
            packed_a.at[r], xa.at[0, opposite(r)], one_send.at[3],
            plane_recv.at[2, r // PART], r_dev(r),
        ).start()
    xa[0, 0] = packed_a[0]
    for k in range(1, NZ):
        remote(codes.at[0], codes.at[NZ - k], one_send.at[2], one_recv.at[0], z_dev(k)).start()
    hand_act = remote(act, before, one_send.at[9], one_recv.at[3], (ahead, e))
    hand_code = remote(codes.at[0], codes.at[NZ], one_send.at[10], one_recv.at[4], (ahead, e))

    def send_packed(i, place):
        packed_b[i] = pack(place, gathered[i]).reshape(NR, CAP, cb)
        for r in range(1, NR):
            remote(
                packed_b.at[i, r], xb.at[i, opposite(r)],
                one_send.at[4], plane_recv.at[0, i], r_dev(r),
            ).start()
        xb[i, 0] = packed_b[i, 0]

    def place_of(i):
        k = [d for d in range(-3, 5) if ZI[d] == i][0]
        return placing((-k) % NZ)

    def arrive(group):
        first = max(1, group * PART)
        drain(xa.at[0, pl.ds(first, (group + 1) * PART - first)], plane_recv.at[2, group])
        begin(group)

    def packs(*blocks):
        for i in blocks:
            send_packed(i, place_of(i))

    def first_half(i, n):
        rows = n * ROWS
        for c in range(0, width, CHUNK):
            if c < CA:
                block = xa[i:i + n, :, :, c:c + CHUNK]
            else:
                block = xb[i:i + n, :, :, c - CA:c - CA + CHUNK]
            term = jnp.dot(
                block.reshape(rows, CHUNK), w1[c:c + CHUNK, :],
                preferred_element_type=jnp.float32,
            )
            if c == 0:
                pre[0:rows, :] = term
            else:
                pre[0:rows, :] += term
        return jax.nn.gelu(pre[0:rows, :], approximate=True).astype(jnp.bfloat16)

    def second_half(hidden, at):
        return jnp.dot(hidden, w2[:, at:at + CHUNK], preferred_element_type=jnp.float32)

    def returns(*blocks):
        for j in blocks:
            for r in range(1, NR):
                remote(
                    back_b.at[j, r], ret_b.at[j, opposite(r)],
                    one_send.at[5], plane_recv.at[1, j], r_dev(r),
                ).start()
            ret_b[j, 0] = back_b[j, 0]

    def run(i, n, at_once=False):
        for j in range(i, i + n):
            drain(xb.at[j, pl.ds(1, NR - 1)], plane_recv.at[0, j])
        hidden = first_half(i, n)
        for c in range(0, cb, CHUNK):
            back_b[i:i + n, :, :, c:c + CHUNK] = (
                second_half(hidden, CA + c).astype(jnp.bfloat16).reshape(n, NR, CAP, CHUNK)
            )
        if at_once:
            returns(*range(i, i + n))
        for c in range(0, CA, CHUNK):
            own_a[i:i + n, :, c:c + CHUNK] = second_half(hidden, c).reshape(n, ROWS, CHUNK)

    send_packed(0, place_own)
    hand_act.start()
    hand_code.start()
    forward(2, 1)
    arrive(0)
    drain(codes.at[pl.ds(1, NZ - 1)], one_recv.at[0])
    packs(1, 2)
    arrive(1)
    forward(2, 2)
    forward(0, 1)
    packs(3, 4)
    forward(1, 1)
    for load in loads[3:]:
        load.wait()
    run(0, 1)
    forward(2, 3)
    packs(5, 6)
    forward(0, 2)
    forward(1, 2)
    run(1, 2)
    forward(2, 4)
    packs(7)
    forward(0, 3)
    forward(1, 3)
    run(3, 2, True)
    forward(0, 4)
    forward(1, 4)

    def rs_copy(kind, d, h, k):
        chain = CHAINS.index((d, h))
        last_b = kind == GROUPS and k == 1
        if kind < GROUPS:
            src, dst = send_a.at[kind, chain, k - 1], land_a.at[kind, chain, k - 1]
        else:
            src, dst = send_b.at[chain, k - 1], land_b.at[chain, k - 1]
        return remote(
            src, dst, one_send.at[6 + kind // GROUPS], rs_recv.at[kind, chain, k - 1],
            z_dev(-d, ahead if last_b else s),
        )

    def rs_own(kind, d, h, k):
        if kind < GROUPS:
            rows = pl.ds(kind * PART * CAP, PART * CAP)
            return own_a[ZI[d * k], rows, h * CA // 2:(h + 1) * CA // 2]
        return own_b[ZI[d * k], :, h * cb // 2:(h + 1) * cb // 2]

    def rs_landed(kind, d, h, k):
        rs_copy(kind, d, h, k + 1).wait_recv()
        chain = CHAINS.index((d, h))
        land = land_a[kind, chain, k] if kind < GROUPS else land_b[chain, k]
        return land.astype(jnp.float32)

    def rs_step(kind, far, k):
        for d, h in CHAINS:
            if FAR[d, h] == far:
                total = rs_own(kind, d, h, k)
                if k < far:
                    total = total + rs_landed(kind, d, h, k)
                total = total.astype(jnp.bfloat16)
                chain = CHAINS.index((d, h))
                if kind < GROUPS:
                    send_a[kind, chain, k - 1] = total
                else:
                    send_b[chain, k - 1] = total
                rs_copy(kind, d, h, k).start()

    def rs_last(kind, h):
        return rs_landed(kind, 1, h, 0) + rs_landed(kind, -1, h, 0)

    def take_b(i):
        drain(ret_b.at[i, pl.ds(1, NR - 1)], plane_recv.at[1, i])
        own_b[i] = unpack(place_of(i), ret_b[i].reshape(ROWS, cb))

    def takes(*blocks):
        for i in blocks:
            take_b(i)

    def return_a(g):
        half = CA // 2
        for h in range(2):
            sum_a[g * PART:(g + 1) * PART, :, h * half:(h + 1) * half] = (
                rs_own(g, 1, h, 0) + rs_last(g, h)
            ).astype(jnp.bfloat16).reshape(PART, CAP, half)
        for r in range(g * PART, (g + 1) * PART):
            remote(
                sum_a.at[r], ret_a.at[opposite(r)], one_send.at[8], one_recv.at[2],
                r_dev(r, ahead),
            ).start()

    def last_b():
        tail_b[0] = own_b[0].astype(jnp.bfloat16)
        remote(tail_b.at[0], tail_b.at[1], one_send.at[11], one_recv.at[5], (ahead, e)).start()

    def write_a():
        drain(ret_a, one_recv.at[2])
        hand_act.wait_recv()
        hand_code.wait_recv()
        out[:, :CA] = (
            before[:, :CA].astype(jnp.float32)
            + unpack(placing(NZ), ret_a[...].reshape(ROWS, CA))
        ).astype(jnp.bfloat16)

    def write_b():
        drain(tail_b.at[1], one_recv.at[5])
        half = cb // 2
        for h in range(2):
            at = slice(CA + h * half, CA + (h + 1) * half)
            out[:, at] = (
                before[:, at].astype(jnp.float32)
                + tail_b[1, :, h * half:(h + 1) * half].astype(jnp.float32)
                + rs_last(GROUPS, h)
            ).astype(jnp.bfloat16)

    run(5, 2, True)
    rs_step(1, 3, 3)
    rs_step(0, 3, 3)
    run(7, 1, True)
    returns(1, 2, 0)
    rs_step(1, 4, 4)
    rs_step(0, 4, 4)
    rs_step(1, 3, 2)
    rs_step(0, 3, 2)
    rs_step(1, 4, 3)
    rs_step(0, 4, 3)
    rs_step(1, 3, 1)
    rs_step(0, 3, 1)
    takes(5, 6)
    rs_step(2, 3, 3)
    rs_step(1, 4, 2)
    rs_step(0, 4, 2)
    takes(7)
    rs_step(2, 4, 4)
    takes(3, 4)
    rs_step(2, 3, 2)
    rs_step(1, 4, 1)
    rs_step(0, 4, 1)
    rs_step(2, 4, 3)
    return_a(1)
    return_a(0)
    takes(1, 2)
    rs_step(2, 3, 1)
    rs_step(2, 4, 2)
    takes(0)
    last_b()
    rs_step(2, 4, 1)
    write_a()
    write_b()

    drain(xa.at[pl.ds(1, NZ - 1)], one_send.at[0])
    drain(gathered.at[pl.ds(1, NZ - 1)], one_send.at[1])
    drain(codes.at[pl.ds(1, NZ - 1)], one_send.at[2])
    drain(packed_a.at[pl.ds(1, NR - 1)], one_send.at[3])
    drain(packed_b.at[:, pl.ds(1, NR - 1)], one_send.at[4])
    drain(back_b.at[:, pl.ds(1, NR - 1)], one_send.at[5])
    drain(xa.at[pl.ds(1, NZ - 1)], one_send.at[6])
    drain(gathered.at[pl.ds(1, NZ - 1)], one_send.at[7])
    drain(sum_a, one_send.at[8])
    drain(tail_b.at[0], one_send.at[11])
    hand_act.wait_send()
    hand_code.wait_send()


def per_device(activations, norm_gain, in_proj, out_proj, expert_ids):
    _, tokens, width = activations.shape
    hidden = in_proj.shape[2]
    cb = width - CA
    bf16, f32 = jnp.bfloat16, jnp.float32
    vmem = pl.BlockSpec(memory_space=pltpu.VMEM)
    hbm = pl.BlockSpec(memory_space=pltpu.HBM)
    out = pl.pallas_call(
        kernel,
        out_shape=jax.ShapeDtypeStruct((tokens, width), bf16),
        in_specs=[hbm] * 5,
        out_specs=vmem,
        scratch_shapes=[
            pltpu.VMEM((tokens, width), bf16),
            pltpu.VMEM((1, width), f32),
            pltpu.VMEM((1, tokens), jnp.int32),
            pltpu.VMEM((tokens, width), bf16),
            pltpu.VMEM((width, hidden), bf16),
            pltpu.VMEM((hidden, width), bf16),
            pltpu.VMEM((NZ + 1, 8, 128), jnp.int32),
            pltpu.VMEM((NZ, tokens, cb), bf16),
            pltpu.VMEM((NR, CAP, CA), bf16),
            pltpu.VMEM((NZ, NR, CAP, cb), bf16),
            pltpu.VMEM((NZ, NR, CAP, CA), bf16),
            pltpu.VMEM((NZ, NR, CAP, cb), bf16),
            pltpu.VMEM((2 * ROWS, hidden), f32),
            pltpu.VMEM((NZ, ROWS, CA), f32),
            pltpu.VMEM((NZ, NR, CAP, cb), bf16),
            pltpu.VMEM((NZ, NR, CAP, cb), bf16),
            pltpu.VMEM((NZ, tokens, cb), f32),
            pltpu.VMEM((NR, CAP, CA), bf16),
            pltpu.VMEM((NR, CAP, CA), bf16),
            pltpu.VMEM((2, tokens, cb), bf16),
            pltpu.VMEM((GROUPS, 4, 4, PART * CAP, CA // 2), bf16),
            pltpu.VMEM((GROUPS, 4, 4, PART * CAP, CA // 2), bf16),
            pltpu.VMEM((4, 4, tokens, cb // 2), bf16),
            pltpu.VMEM((4, 4, tokens, cb // 2), bf16),
            pltpu.SemaphoreType.DMA((5,)),
            pltpu.SemaphoreType.DMA((12,)),
            pltpu.SemaphoreType.DMA((6,)),
            pltpu.SemaphoreType.DMA((GROUPS + 1, 4, 4)),
            pltpu.SemaphoreType.DMA((3, NZ)),
            pltpu.SemaphoreType.DMA((GROUPS + 1, 4, 4)),
        ],
        compiler_params=pltpu.CompilerParams(
            collective_id=0, has_side_effects=True, vmem_limit_bytes=58 * 2**20
        ),
    )(activations[0], norm_gain, expert_ids.reshape(1, tokens), in_proj[0], out_proj[0])
    return out[None]


def solution(mesh):
    return jax.shard_map(
        per_device,
        mesh=mesh,
        in_specs=(
            P("section", "expert", None),
            P("section", None),
            P("section", None, "expert"),
            P("section", "expert", None),
            P("section", "expert", None),
        ),
        out_specs=P("section", "expert", None),
        check_vma=False,
    )
```

time: 96.8 us -> 86.1 us (0.89)
  Pallas kernels: 93.6 us -> 84.3 us
  local copies, waits for them, and re-layouts: 3.01 us -> 1.67 us
    pallas_call x1, Pallas kernels: 93.6 us -> 84.3 us  [per_device(): pl.pallas_call(kernel, out_shape=jax.ShapeDtypeStruct((tokens, width), bf...]
    squeeze x1 -> x0, local copies, waits for them, and re-layouts: 1.34 us -> none  [per_device(): expert_ids[0]]
where the time goes in v2:
time: 86.1 us; the launch traced here: 86 us
  Pallas kernels  84.3 us (98%)
  local copies, waits for them, and re-layouts  1.67 us (2%)
    pallas_call x1, Pallas kernels, per_device(): pl.pallas_call(kernel, out_shape=jax.ShapeDtypeStruct((tokens, width), bf...  84.3 us

profile of v2, /device:TPU:1, one launch (start us, length us, event | category | flops | bytes accessed | tf_op | source)
XLA Modules:
  0.0 86.0 jit_solution(14590773271302515468)
XLA Ops:
  0.0 84.3 %shard_map.55 = bf16[32,4096]{1,0:T(8,128)(2,1)} custom-call(bf16[32,4096]{1,0:T(8,128)(2,1)} %bitcast.8, f32[1,4096]{1,0:T(1,128)} %gain_hbm.1, s32[1,32]{1,0:T(1,128)} %bitcast.9, bf16[4096,640]{1,0:T(8,128)(2,1)} %bitcast.5, bf16[640,4096]{1,0:T(8,128)(2,1)} %bitcast.6), custom_call_target="tpu_custom_call" | custom-call | tf_op jit(solution)/shard_map/pallas_call | solution.py:389
  84.3 1.7 %copy.7 = bf16[1,32,4096]{2,1,0:T(8,128)(2,1)} copy(bf16[1,32,4096]{2,1,0:T(8,128)(2,1)} %bitcast.7) | data formatting | bytes 524288

commit v3 on v2

--- a/solution.py
+++ b/solution.py
@@ -133,11 +133,11 @@
         for d, h in CHAINS:
             ag_copy(kind, d, h, 0).start()
 
-    def forward(kind, k):
+    def forward(kind, k, far):
         for d, h in CHAINS:
-            if k <= FAR[d, h]:
+            if FAR[d, h] == far:
                 ag_copy(kind, d, h, k - 1).wait_recv()
-                if k < FAR[d, h]:
+                if k < far:
                     ag_copy(kind, d, h, k).start()
 
     begin(2)
@@ -175,13 +175,13 @@
         for i in blocks:
             send_packed(i, place_of(i))
 
-    def first_half(i, n):
-        rows = n * ROWS
+    def hidden_of(i, j, a=0, b=NR):
+        rows = (j - i) * (b - a) * CAP
         for c in range(0, width, CHUNK):
             if c < CA:
-                block = xa[i:i + n, :, :, c:c + CHUNK]
+                block = xa[i:j, a:b, :, c:c + CHUNK]
             else:
-                block = xb[i:i + n, :, :, c - CA:c - CA + CHUNK]
+                block = xb[i:j, a:b, :, c - CA:c - CA + CHUNK]
             term = jnp.dot(
                 block.reshape(rows, CHUNK), w1[c:c + CHUNK, :],
                 preferred_element_type=jnp.float32,
@@ -192,58 +192,34 @@
                 pre[0:rows, :] += term
         return jax.nn.gelu(pre[0:rows, :], approximate=True).astype(jnp.bfloat16)
 
-    def second_half(hidden, at):
+    def part_of(hidden, at):
         return jnp.dot(hidden, w2[:, at:at + CHUNK], preferred_element_type=jnp.float32)
 
-    def returns(*blocks):
-        for j in blocks:
-            for r in range(1, NR):
+    def columns_b(hidden, i, j, a=0, b=NR):
+        for c in range(0, cb, CHUNK):
+            back_b[i:j, a:b, :, c:c + CHUNK] = (
+                part_of(hidden, CA + c).astype(jnp.bfloat16).reshape(j - i, b - a, CAP, CHUNK)
+            )
+
+    def columns_a(hidden, i, j, a=0, b=NR):
+        for c in range(0, CA, CHUNK):
+            own_a[i:j, a * CAP:b * CAP, c:c + CHUNK] = (
+                part_of(hidden, c).reshape(j - i, (b - a) * CAP, CHUNK)
+            )
+
+    def returns(j, a, b):
+        for r in range(a, b):
+            if r == 0:
+                ret_b[j, 0] = back_b[j, 0]
+            else:
                 remote(
                     back_b.at[j, r], ret_b.at[j, opposite(r)],
                     one_send.at[5], plane_recv.at[1, j], r_dev(r),
                 ).start()
-            ret_b[j, 0] = back_b[j, 0]
-
-    def run(i, n, at_once=False):
-        for j in range(i, i + n):
+
+    def landed(*blocks):
+        for j in blocks:
             drain(xb.at[j, pl.ds(1, NR - 1)], plane_recv.at[0, j])
-        hidden = first_half(i, n)
-        for c in range(0, cb, CHUNK):
-            back_b[i:i + n, :, :, c:c + CHUNK] = (
-                second_half(hidden, CA + c).astype(jnp.bfloat16).reshape(n, NR, CAP, CHUNK)
-            )
-        if at_once:
-            returns(*range(i, i + n))
-        for c in range(0, CA, CHUNK):
-            own_a[i:i + n, :, c:c + CHUNK] = second_half(hidden, c).reshape(n, ROWS, CHUNK)
-
-    send_packed(0, place_own)
-    hand_act.start()
-    hand_code.start()
-    forward(2, 1)
-    arrive(0)
-    drain(codes.at[pl.ds(1, NZ - 1)], one_recv.at[0])
-    packs(1, 2)
-    arrive(1)
-    forward(2, 2)
-    forward(0, 1)
-    packs(3, 4)
-    forward(1, 1)
-    for load in loads[3:]:
-        load.wait()
-    run(0, 1)
-    forward(2, 3)
-    packs(5, 6)
-    forward(0, 2)
-    forward(1, 2)
-    run(1, 2)
-    forward(2, 4)
-    packs(7)
-    forward(0, 3)
-    forward(1, 3)
-    run(3, 2, True)
-    forward(0, 4)
-    forward(1, 4)
 
     def rs_copy(kind, d, h, k):
         chain = CHAINS.index((d, h))
@@ -290,10 +266,6 @@
         drain(ret_b.at[i, pl.ds(1, NR - 1)], plane_recv.at[1, i])
         own_b[i] = unpack(place_of(i), ret_b[i].reshape(ROWS, cb))
 
-    def takes(*blocks):
-        for i in blocks:
-            take_b(i)
-
     def return_a(g):
         half = CA // 2
         for h in range(2):
@@ -330,37 +302,108 @@
                 + rs_last(GROUPS, h)
             ).astype(jnp.bfloat16)
 
-    run(5, 2, True)
+    send_packed(0, place_own)
+    hand_act.start()
+    hand_code.start()
+    forward(2, 1, 4)
+    forward(2, 1, 3)
+    drain(codes.at[pl.ds(1, NZ - 1)], one_recv.at[0])
+    arrive(0)
+    packs(2)
+    forward(2, 2, 3)
+    forward(2, 2, 4)
+    packs(4)
+    arrive(1)
+    packs(3)
+    forward(2, 3, 4)
+    forward(2, 3, 3)
+    packs(6)
+    forward(1, 1, 4)
+    forward(0, 1, 3)
+    forward(0, 1, 4)
+    packs(5)
+    forward(2, 4, 4)
+    for load in loads[3:]:
+        load.wait()
+    landed(0)
+    h0101 = hidden_of(0, 1, 0, NR)
+    packs(7)
+    forward(1, 2, 4)
+    forward(1, 1, 3)
+    columns_b(h0101, 0, 1, 0, NR)
+    packs(1)
+    forward(0, 2, 4)
+    forward(1, 3, 4)
+    forward(1, 2, 3)
+    returns(0, 0, PART)
+    forward(0, 2, 3)
+    landed(3, 4)
+    h3501 = hidden_of(3, 5, 0, NR)
+    columns_b(h3501, 3, 5, 0, NR)
+    forward(0, 3, 4)
+    returns(3, PART, NR)
+    returns(3, 0, PART)
+    forward(1, 4, 4)
+    returns(0, PART, NR)
+    forward(1, 3, 3)
+    landed(5, 6, 7)
+    h581 = hidden_of(5, 8, PART, NR)
+    columns_a(h581, 5, 8, PART, NR)
+    rs_step(1, 4, 4)
     rs_step(1, 3, 3)
+    forward(0, 4, 4)
+    returns(4, PART, NR)
+    forward(0, 3, 3)
+    h580 = hidden_of(5, 8, 0, PART)
+    columns_a(h580, 5, 8, 0, PART)
+    rs_step(0, 4, 4)
+    columns_b(h581, 5, 8, PART, NR)
     rs_step(0, 3, 3)
-    run(7, 1, True)
-    returns(1, 2, 0)
-    rs_step(1, 4, 4)
-    rs_step(0, 4, 4)
-    rs_step(1, 3, 2)
-    rs_step(0, 3, 2)
+    columns_b(h580, 5, 8, 0, PART)
+    returns(5, 0, PART)
+    returns(7, PART, NR)
+    returns(7, 0, PART)
     rs_step(1, 4, 3)
     rs_step(0, 4, 3)
+    returns(6, PART, NR)
+    columns_a(h3501, 3, 5, 0, NR)
+    rs_step(1, 3, 2)
+    returns(6, 0, PART)
+    rs_step(0, 3, 2)
+    take_b(3)
+    rs_step(1, 4, 2)
+    landed(1, 2)
+    h1301 = hidden_of(1, 3, 0, NR)
+    returns(5, PART, NR)
+    columns_b(h1301, 1, 3, 0, NR)
+    returns(1, PART, NR)
+    rs_step(0, 4, 2)
+    returns(4, 0, PART)
+    returns(1, 0, PART)
+    columns_a(h1301, 1, 3, 0, NR)
+    returns(2, PART, NR)
     rs_step(1, 3, 1)
+    take_b(7)
+    rs_step(1, 4, 1)
+    rs_step(2, 4, 4)
+    take_b(0)
+    take_b(6)
     rs_step(0, 3, 1)
-    takes(5, 6)
+    returns(2, 0, PART)
+    take_b(5)
     rs_step(2, 3, 3)
-    rs_step(1, 4, 2)
-    rs_step(0, 4, 2)
-    takes(7)
-    rs_step(2, 4, 4)
-    takes(3, 4)
-    rs_step(2, 3, 2)
-    rs_step(1, 4, 1)
-    rs_step(0, 4, 1)
+    columns_a(h0101, 0, 1, 0, NR)
     rs_step(2, 4, 3)
     return_a(1)
+    last_b()
+    take_b(4)
+    rs_step(0, 4, 1)
+    rs_step(2, 3, 2)
+    take_b(1)
+    rs_step(2, 4, 2)
     return_a(0)
-    takes(1, 2)
+    take_b(2)
     rs_step(2, 3, 1)
-    rs_step(2, 4, 2)
-    takes(0)
-    last_b()
     rs_step(2, 4, 1)
     write_a()
     write_b()

time: 86.1 us -> 81.2 us (0.943)
  Pallas kernels: 84.3 us -> 79.4 us
    pallas_call x1, Pallas kernels: 84.3 us -> 79.4 us  [per_device(): pl.pallas_call(kernel, out_shape=jax.ShapeDtypeStruct((tokens, width), bf...]
where the time goes in v3:
time: 81.2 us; the launch traced here: 81.1 us
  Pallas kernels  79.4 us (98%)
  local copies, waits for them, and re-layouts  1.67 us (2%)
    pallas_call x1, Pallas kernels, per_device(): pl.pallas_call(kernel, out_shape=jax.ShapeDtypeStruct((tokens, width), bf...  79.4 us
    unnamed x1, local copies, waits for them, and re-layouts  1.67 us

profile of v3, /device:TPU:1, one launch (start us, length us, event | category | flops | bytes accessed | tf_op | source)
XLA Modules:
  0.0 81.1 jit_solution(3959846365135480832)
XLA Ops:
  0.0 79.4 %shard_map.55 = bf16[32,4096]{1,0:T(8,128)(2,1)} custom-call(bf16[32,4096]{1,0:T(8,128)(2,1)} %bitcast.8, f32[1,4096]{1,0:T(1,128)} %gain_hbm.1, s32[1,32]{1,0:T(1,128)} %bitcast.9, bf16[4096,640]{1,0:T(8,128)(2,1)} %bitcast.5, bf16[640,4096]{1,0:T(8,128)(2,1)} %bitcast.6), custom_call_target="tpu_custom_call" | custom-call | tf_op jit(solution)/shard_map/pallas_call | solution.py:432
  79.4 1.7 %copy.7 = bf16[1,32,4096]{2,1,0:T(8,128)(2,1)} copy(bf16[1,32,4096]{2,1,0:T(8,128)(2,1)} %bitcast.7) | data formatting | bytes 524288

commit v4 on v3

--- a/solution.py
+++ b/solution.py
@@ -303,8 +303,6 @@
             ).astype(jnp.bfloat16)
 
     send_packed(0, place_own)
-    hand_act.start()
-    hand_code.start()
     forward(2, 1, 4)
     forward(2, 1, 3)
     drain(codes.at[pl.ds(1, NZ - 1)], one_recv.at[0])
@@ -328,6 +326,8 @@
     landed(0)
     h0101 = hidden_of(0, 1, 0, NR)
     packs(7)
+    hand_act.start()
+    hand_code.start()
     forward(1, 2, 4)
     forward(1, 1, 3)
     columns_b(h0101, 0, 1, 0, NR)

time: 81.2 us -> 80.6 us (level)
  no operation moved by 1% of the time
where the time goes in v4:
time: 80.6 us; the launch traced here: 80.5 us
  Pallas kernels  78.9 us (98%)
  local copies, waits for them, and re-layouts  1.67 us (2%)
    pallas_call x1, Pallas kernels, per_device(): pl.pallas_call(kernel, out_shape=jax.ShapeDtypeStruct((tokens, width), bf...  78.9 us
    unnamed x1, local copies, waits for them, and re-layouts  1.67 us

profile of v4, /device:TPU:1, one launch (start us, length us, event | category | flops | bytes accessed | tf_op | source)
XLA Modules:
  0.0 80.5 jit_solution(17407806621143313845)
XLA Ops:
  0.0 78.9 %shard_map.55 = bf16[32,4096]{1,0:T(8,128)(2,1)} custom-call(bf16[32,4096]{1,0:T(8,128)(2,1)} %bitcast.8, f32[1,4096]{1,0:T(1,128)} %gain_hbm.1, s32[1,32]{1,0:T(1,128)} %bitcast.9, bf16[4096,640]{1,0:T(8,128)(2,1)} %bitcast.5, bf16[640,4096]{1,0:T(8,128)(2,1)} %bitcast.6), custom_call_target="tpu_custom_call" | custom-call | tf_op jit(solution)/shard_map/pallas_call | solution.py:432
  78.9 1.7 %copy.7 = bf16[1,32,4096]{2,1,0:T(8,128)(2,1)} copy(bf16[1,32,4096]{2,1,0:T(8,128)(2,1)} %bitcast.7) | data formatting | bytes 524288
